TPU v7x, 32 devices: a whole 2x2x4 slice. The times are simulated.
32 devices in a mesh: dp: 4 (over z), ep: 8 (over y, x, core).
Axes of the slice: x: 2, y: 2, z: 4, core: 2. Of those that a mesh axis runs over, the one named last changes fastest.
Arguments:
- hidden: bfloat16 [8192, 1280], P(('dp', 'ep')), parts along dimension 0
- norm_gain: float32 [1280], replicated
- router_w: bfloat16 [1280, 64], replicated
- topk_idx: int32 [8192, 6], P(('dp', 'ep')), parts along dimension 0
- w_gate: bfloat16 [64, 1280, 896], P('ep')
- w_up: bfloat16 [64, 1280, 896], P('ep')
- w_down: bfloat16 [64, 896, 1280], P('ep')
- shared_gate: bfloat16 [1280, 1792], replicated
- shared_up: bfloat16 [1280, 1792], replicated
- shared_down: bfloat16 [1792, 1280], replicated
Outputs:
- output: bfloat16 [8192, 1280], P(('dp', 'ep')), parts along dimension 0
There are 4 independent parts. A program takes and returns all parts, laid end to end along the dimension named above; an argument that names none is the same for every part.
All inputs are finite; a program needn't handle non-finite values.
Results may differ from a plain program's by a relative error of at most 0.001.
Values are sent between devices in bfloat16 or wider.
A program may use at most 1 GiB of HBM per device.

v0:
```python
import jax
import jax.numpy as jnp
from jax import lax
from jax.sharding import PartitionSpec as P

NORM_EPS = 1e-6


def rms_norm(hidden, norm_gain):
    hidden_f32 = hidden.astype(jnp.float32)
    inv_rms = lax.rsqrt(jnp.mean(hidden_f32 * hidden_f32, axis=-1, keepdims=True) + NORM_EPS)
    return (hidden_f32 * inv_rms * norm_gain).astype(jnp.bfloat16)


def shared_swiglu(normed, shared_gate, shared_up, shared_down):
    gate_out = jnp.dot(normed, shared_gate, preferred_element_type=jnp.float32)
    up_out = jnp.dot(normed, shared_up, preferred_element_type=jnp.float32)
    activated = (jax.nn.silu(gate_out) * up_out).astype(jnp.bfloat16)
    return jnp.dot(activated, shared_down, preferred_element_type=jnp.float32)


def route_weights(normed, router_w, topk_idx):
    logits = jnp.dot(normed, router_w, preferred_element_type=jnp.float32)
    return jnp.take_along_axis(jax.nn.softmax(logits, axis=-1), topk_idx, axis=1)


def route_layout(topk_idx, num_experts, capacity, group_size):
    tok_count, top_k = topk_idx.shape
    row_count = tok_count * top_k
    local_count = num_experts // group_size
    flat_expert = topk_idx.reshape(-1)
    row_order = jnp.argsort(flat_expert, stable=True)
    sorted_expert = flat_expert[row_order]
    counts = jnp.zeros((num_experts,), jnp.int32).at[flat_expert].add(1)
    rank_sorted = jnp.arange(row_count) - (jnp.cumsum(counts) - counts)[sorted_expert]
    slot_sorted = ((sorted_expert % local_count) * group_size + sorted_expert // local_count) * capacity + rank_sorted
    row_slot = jnp.zeros((row_count,), jnp.int32).at[row_order].set(slot_sorted)
    slot_token = jnp.full((num_experts * capacity,), tok_count, jnp.int32).at[slot_sorted].set(row_order // top_k)
    return row_slot, slot_token


def expert_swiglu(expert_in, w_gate, w_up, w_down):
    gate_out = jnp.einsum('ech,ehi->eci', expert_in, w_gate, preferred_element_type=jnp.float32)
    up_out = jnp.einsum('ech,ehi->eci', expert_in, w_up, preferred_element_type=jnp.float32)
    activated = (jax.nn.silu(gate_out) * up_out).astype(jnp.bfloat16)
    return jnp.einsum('eci,eih->ech', activated, w_down, preferred_element_type=jnp.float32).astype(jnp.bfloat16)


def finish_output(hidden, shared_out, row_out, route_w):
    routed = jnp.sum(row_out.astype(jnp.float32) * route_w[:, :, None], axis=1)
    return (hidden.astype(jnp.float32) + shared_out + routed).astype(jnp.bfloat16)


def solution(mesh):
    group_size = mesh.shape['ep']

    def local_step(hidden, norm_gain, router_w, topk_idx, w_gate, w_up, w_down, shared_gate, shared_up, shared_down):
        tok_count, hidden_size = hidden.shape
        top_k = topk_idx.shape[1]
        num_experts = router_w.shape[1]
        local_count = w_gate.shape[0]
        capacity = 3 * tok_count * top_k // (2 * num_experts)
        normed = rms_norm(hidden, norm_gain)
        route_w = route_weights(normed, router_w, topk_idx)
        row_slot, slot_token = route_layout(topk_idx, num_experts, capacity, group_size)
        normed_pad = jnp.concatenate([normed, jnp.zeros((1, hidden_size), normed.dtype)], axis=0)
        send_buf = normed_pad[slot_token].reshape(local_count, group_size, capacity, hidden_size)
        recv_buf = lax.all_to_all(send_buf, 'ep', 1, 1, tiled=True)
        expert_out = expert_swiglu(recv_buf.reshape(local_count, group_size * capacity, hidden_size), w_gate, w_up, w_down)
        back_buf = lax.all_to_all(expert_out.reshape(local_count, group_size, capacity, hidden_size), 'ep', 1, 1, tiled=True)
        shared_out = shared_swiglu(normed, shared_gate, shared_up, shared_down)
        row_out = back_buf.reshape(local_count * group_size * capacity, hidden_size)[row_slot]
        return finish_output(hidden, shared_out, row_out.reshape(tok_count, top_k, hidden_size), route_w)

    token_spec = P(('dp', 'ep'), None)
    expert_spec = P('ep', None, None)
    return jax.shard_map(
        local_step,
        mesh=mesh,
        in_specs=(token_spec, P(None), P(None, None), token_spec, expert_spec, expert_spec, expert_spec,
                  P(None, None), P(None, None), P(None, None)),
        out_specs=token_spec,
        check_vma=False,
    )
```

profile of v0, /device:TPU:0, one launch (start us, length us, event | category | flops | bytes accessed | tf_op | source)
XLA Modules:
  0.0 347.9 jit_solution(1277465128378482366)
XLA Ops:
  0.0 0.0 copy-start
  0.0 0.9 copy.38
  0.9 0.1 reshape.207
  1.0 0.1 reshape.206
  1.2 11.1 %scatter_custom_fusion = s32[64]{0:T(128)S(1)} fusion(s32[1536]{0:T(1024)S(1)} %fusion.27, s32[1536]{0:T(1024)S(1)} %broadcast.325, s32[]{:T(128)} %constant.72.clone.1), kind=kCustom, calls=%fused_computation.137 | custom fusion | flops 1536 | bytes 260 | tf_op jit(solution)/shard_map/scatter-add | solution.py:34
  12.3 0.1 copy.40
  12.4 0.1 reduce-window.9
  12.5 0.1 reduce.2
  12.7 0.7 fusion.48
  13.4 0.7 fusion.45
  14.1 0.7 fusion.46
  14.8 0.7 fusion.47
  15.6 5.0 %sort.17 = (s32[1536]{0:T(1024)}, s32[1536]{0:T(1024)S(1)}) sort(s32[1536]{0:T(1024)S(1)} %reshape.206, s32[1536]{0:T(1024)S(1)} %iota.10), dimensions={0}, to_apply=%region_1.0 | sort | flops 16896 | bytes 24576 | tf_op jit(solution)/shard_map/jit(argsort)/sort | solution.py:32
  20.6 0.0 copy-start.3
  20.6 0.0 copy-start.5
  20.6 8.4 %gather_fusion = s32[1536]{0:T(1024)S(1)} fusion(s32[1536]{0:T(1024)S(1)} %reshape.206, s32[2048]{0:T(1024)S(1)} %pad_clamp_fusion.2), kind=kCustom, calls=%fused_computation | custom fusion | bytes 18432 | tf_op jit(solution)/shard_map/gather | solution.py:33
  29.0 4.3 %fusion.26 = (s32[1536]{0:T(1024)S(1)}, s32[1536,1]{0,1:T(1,128)S(1)}) fusion(s32[]{:T(128)} %bitcast.58, s32[]{:T(128)} %bitcast.59, s32[]{:T(128)} %bitcast.60, s32[]{:T(128)} %bitcast.61, s32[]{:T(128)} %bitcast.62, s32[]{:T(128)} %bitcast.64, s32[]{:T(128)} %bitcast.63, s32[1536]{0:T(1024)S(1)} %gather_fusion), kind=kLoop, calls=%fused_computation.127 | loop fusion | flops 23040 | bytes 18460 | tf_op jit(solution)/shard_map/gather | solution.py:35
  33.4 1.1 compare_reduce_fusion.56
  34.5 35.7 %fusion.20 = (s32[1536]{0:T(1024)S(1)}, s32[1536]{0:T(1024)S(1)}) fusion(s32[1536]{0:T(1024)S(1)} %gather_fusion, pred[1536]{0:T(1024)(128)(4,1)S(1)} %get-tuple-element.63, pred[1536]{0:T(1024)(128)(4,1)S(1)} %get-tuple-element.62, pred[1536]{0:T(1024)(128)(4,1)S(1)} %get-tuple-element.61, pred[1536]{0:T(1024)(128)(4,1)S(1)} %get-tuple-element.60, ...), kind=kLoop, calls=%fused_computation.113 | loop fusion | flops 124416 | bytes 112356 | tf_op jit(solution)/shard_map/add | solution.py:36
  70.2 0.1 fusion.28
  70.2 6.2 %scatter_custom_fusion.1 = s32[2304]{0:T(1024)S(1)} fusion(s32[1536]{0:T(1024)S(1)} %fusion.28, s32[1536]{0:T(1024)S(1)} %get-tuple-element.68, s32[]{:T(128)} %constant.71.clone.1), kind=kCustom, calls=%fused_computation.132 | custom fusion | bytes 9220 | tf_op jit(solution)/shard_map/scatter | solution.py:38
  76.5 0.0 copy-done.3
  76.5 0.2 fusion.12
  76.7 0.0 copy-done.5
  76.7 0.2 fusion.14
  77.0 8.5 %gather_fusion.1 = bf16[2304,1280]{1,0:T(8,128)(2,1)} fusion(bf16[257,1280]{1,0:T(8,128)(2,1)S(1)} %concatenate.3, s32[3072]{0:T(1024)S(1)} %pad_clamp_fusion), kind=kCustom, calls=%fused_computation.1 | custom fusion | bytes 11805696 | tf_op jit(solution)/shard_map/gather | solution.py:67
  85.5 9.2 %reshape.210 = bf16[8,8,36,1280]{3,2,1,0:T(8,128)(2,1)} reshape(bf16[2304,1280]{1,0:T(8,128)(2,1)} %gather_fusion.1) | data formatting | bytes 11796480 | tf_op jit(solution)/shard_map/reshape | solution.py:67
  94.7 6.1 %copy.41 = bf16[8,8,36,1280]{3,0,2,1:T(8,128)(2,1)S(1)} copy(bf16[8,8,36,1280]{3,2,1,0:T(8,128)(2,1)} %reshape.210) | data formatting | bytes 11796480 | tf_op jit(solution)/shard_map/reshape | solution.py:67
  100.8 72.3 %all_to_all.10 = bf16[8,8,36,1280]{3,0,2,1:T(8,128)(2,1)S(1)} all-to-all(bf16[8,8,36,1280]{3,0,2,1:T(8,128)(2,1)S(1)} %copy.41), channel_id=1, replica_groups=mesh['dp'=4,'ep'=8] {'ep'}, dimensions={1} | all-to-all | bytes 11796480 | tf_op jit(solution)/shard_map/all_to_all | solution.py:68
  173.1 0.0 copy-start.2
  173.1 2.5 copy-done.2
  175.6 12.0 %fusion = f32[8,288,896]{2,1,0:T(8,128)} fusion(bf16[8,1280,896]{2,1,0:T(8,128)(2,1)} %param.15, bf16[8,288,1280]{2,0,1:T(8,128)(2,1)S(1)} %bitcast.79), kind=kOutput, calls=%fused_computation.10 | convolution fusion | flops 5284823040 | bytes 32505856 | tf_op jit(solution)/shard_map/ech,ehi->eci/dot_general | solution.py:44
  187.6 28.6 %convolution_convert_fusion = bf16[8,288,1280]{2,1,0:T(8,128)(2,1)} fusion(bf16[8,896,1280]{2,1,0:T(8,128)(2,1)} %param.16, f32[8,288,896]{2,1,0:T(8,128)} %fusion, bf16[8,1280,896]{2,1,0:T(8,128)(2,1)} %param.14, bf16[8,288,1280]{2,0,1:T(8,128)(2,1)} %bitcast.80), kind=kOutput, calls=%fused_computation.9 | convolution fusion | flops 10584981504 | bytes 56754176 | tf_op jit(solution)/shard_map/eci,eih->ech/dot_general | solution.py:46
  216.2 8.4 %copy.44 = bf16[8,288,1280]{2,0,1:T(8,128)(2,1)} copy(bf16[8,288,1280]{2,1,0:T(8,128)(2,1)} %convolution_convert_fusion) | data formatting | bytes 11796480 | tf_op jit(solution)/shard_map/convert_element_type | solution.py:46
  224.7 0.0 copy-start.4
  224.7 4.9 %all-to-all-start.1 = ((bf16[8,8,36,1280]{3,0,2,1:T(8,128)(2,1)}), bf16[8,8,36,1280]{3,0,2,1:T(8,128)(2,1)}, u32[]{:S(2)}, u32[]{:S(2)}) async-start(bf16[8,8,36,1280]{3,0,2,1:T(8,128)(2,1)} %bitcast.78), calls=%async_computation.1 | async-start | bytes 11796480 | tf_op jit(solution)/shard_map/all_to_all | solution.py:70
  229.5 6.4 %scatter_custom_fusion.2 = s32[1536]{0:T(1024)S(1)} fusion(s32[1536]{0:T(1024)S(1)} %get-tuple-element.69, s32[1536]{0:T(1024)S(1)} %get-tuple-element.64, s32[]{:T(128)} %constant.72.clone.1), kind=kCustom, calls=%fused_computation.134 | custom fusion | bytes 6148 | tf_op jit(solution)/shard_map/scatter | solution.py:37
  236.0 0.0 copy-done.4
  236.0 0.1 copy.46
  236.1 0.1 reshape.311
  236.3 0.0 copy-done
  236.3 0.4 fusion.49
  236.8 12.7 %gather_fusion.3 = f32[1536]{0:T(1024)S(1)} fusion(f32[256,64]{0,1:T(8,128)S(1)} %fusion.15, s32[1536]{0:T(1024)S(1)} %reshape.311), kind=kCustom, calls=%fused_computation.3 | custom fusion | bytes 24576 | tf_op jit(solution)/shard_map/jit(take_along_axis)/gather | solution.py:24
  249.5 0.1 reshape.314
  249.7 0.1 copy.47
  249.7 0.1 copy.48
  249.9 5.0 %fusion.43 = f32[256,1792]{1,0:T(8,128)} fusion(bf16[1280,1792]{1,0:T(8,128)(2,1)} %param.17, bf16[256,1280]{1,0:T(8,128)(2,1)S(1)} %copy-done.3, f32[1280]{0:T(1024)S(1)} %copy-done.5, f32[256]{0:T(256)S(1)} %add_rsqrt_fusion), kind=kOutput, calls=%fused_computation.142 | convolution fusion | flops 1175715840 | bytes 7084032 | tf_op jit(solution)/shard_map/dot_general | solution.py:16
  254.9 41.9 %all-to-all-done.1 = bf16[8,8,36,1280]{3,0,2,1:T(8,128)(2,1)} async-done(((bf16[8,8,36,1280]{3,0,2,1:T(8,128)(2,1)}), bf16[8,8,36,1280]{3,0,2,1:T(8,128)(2,1)}, u32[]{:S(2)}, u32[]{:S(2)}) %all-to-all-start.1) | async-done | bytes 5898272 | tf_op jit(solution)/shard_map/all_to_all | solution.py:70
  296.8 6.6 %copy.45 = bf16[8,8,36,1280]{3,2,1,0:T(8,128)(2,1)} copy(bf16[8,8,36,1280]{3,0,2,1:T(8,128)(2,1)} %all-to-all-done.1) | data formatting | bytes 11796480 | tf_op jit(solution)/shard_map/all_to_all | solution.py:70
  303.4 9.2 %reshape.213 = bf16[2304,1280]{1,0:T(8,128)(2,1)} reshape(bf16[8,8,36,1280]{3,2,1,0:T(8,128)(2,1)} %copy.45) | data formatting | bytes 11796480 | tf_op jit(solution)/shard_map/reshape | solution.py:72
  312.6 12.4 %gather_fusion.2 = bf16[1536,1280]{1,0:T(8,128)(2,1)} fusion(bf16[2304,1280]{1,0:T(8,128)(2,1)} %reshape.213, s32[2048]{0:T(1024)S(1)} %pad_clamp_fusion.1), kind=kCustom, calls=%fused_computation.2 | custom fusion | bytes 7870464 | tf_op jit(solution)/shard_map/gather | solution.py:72
  325.0 7.7 %reshape.215 = f32[256,6,1280]{2,1,0:T(8,128)} reshape(bf16[1536,1280]{1,0:T(8,128)(2,1)} %gather_fusion.2) | data formatting | bytes 11796480 | tf_op jit(solution)/shard_map/convert_element_type | solution.py:50
  332.8 7.3 %multiply_reduce_fusion = f32[256,1280]{1,0:T(8,128)S(1)} fusion(f32[256,6,1280]{2,1,0:T(8,128)} %reshape.215, f32[256,6]{1,0:T(8,128)S(1)} %copy.48), kind=kLoop, calls=%fused_computation.7 | loop fusion | flops 3604480 | bytes 9181184 | tf_op jit(solution)/shard_map/reduce_sum | solution.py:50
  340.0 0.0 copy-start.1
  340.1 7.8 %fusion.10 = bf16[256,1280]{1,0:T(8,128)(2,1)} fusion(f32[256,1280]{1,0:T(8,128)S(1)} %multiply_reduce_fusion, bf16[1792,1280]{1,0:T(8,128)(2,1)} %param.19, bf16[256,1280]{1,0:T(8,128)(2,1)S(1)} %copy-done.3, bf16[1280,1792]{1,0:T(8,128)(2,1)} %param.18, f32[256,1792]{1,0:T(8,128)} %fusion.43, f32[1280]{0:T(1024)S(1)} %copy-done.5, f32[256]{0:T(256)S(1)} %add_rsqrt_fusion), kind=kOutput, calls=%fused_computation.18 | convolution fusion | flops 2354184192 | bytes 13637632 | tf_op jit(solution)/shard_map/dot_general | solution.py:19
  347.9 0.0 copy-done.1
  (16 shorter events, 0.2 us)
Async XLA Ops:
  0.0 236.3 %copy-start = (bf16[1280,64]{0,1:T(8,128)(2,1)S(1)}, bf16[1280,64]{0,1:T(8,128)(2,1)}, u32[]{:S(2)}) copy-start(bf16[1280,64]{0,1:T(8,128)(2,1)} %param.12) | copy-start | bytes 491524
  20.6 55.9 %copy-start.3 = (bf16[256,1280]{1,0:T(8,128)(2,1)S(1)}, bf16[256,1280]{1,0:T(8,128)(2,1)}, u32[]{:S(2)}) copy-start(bf16[256,1280]{1,0:T(8,128)(2,1)} %param.10) | copy-start | bytes 1966084
  20.6 56.1 %copy-start.5 = (f32[1280]{0:T(1024)S(1)}, f32[1280]{0:T(1024)}, u32[]{:S(2)}) copy-start(f32[1280]{0:T(1024)} %param.11) | copy-start | bytes 15364
  173.1 2.5 copy-start.2
  224.7 11.3 %copy-start.4 = (s32[256,6]{0,1:T(8,128)S(1)}, s32[256,6]{0,1:T(8,128)}, u32[]{:S(2)}) copy-start(s32[256,6]{0,1:T(8,128)} %param.13) | copy-start | bytes 18436
  224.7 72.1 %all-to-all-start.1 = ((bf16[8,8,36,1280]{3,0,2,1:T(8,128)(2,1)}), bf16[8,8,36,1280]{3,0,2,1:T(8,128)(2,1)}, u32[]{:S(2)}, u32[]{:S(2)}) async-start(bf16[8,8,36,1280]{3,0,2,1:T(8,128)(2,1)} %bitcast.78), calls=%async_computation.1 | async-start | bytes 11796480 | tf_op jit(solution)/shard_map/all_to_all | solution.py:70
  340.0 7.8 %copy-start.1 = (bf16[1280,64]{0,1:T(8,128)(2,1)S(1)}, bf16[1280,64]{0,1:T(8,128)(2,1)}, u32[]{:S(2)}) copy-start(bf16[1280,64]{0,1:T(8,128)(2,1)} %param.12) | copy-start | bytes 491524
where the time goes:
time: 349 us; the launch traced here: 348 us
  local copies, waits for them, and re-layouts  109 us (31%)
  blocking collectives  72.3 us (21%)
  other arithmetic  65.4 us (19%)
  matrix products  53.8 us (15%)
  waiting for transfers between devices  41.9 us (12%)
  starting transfers between devices  4.86 us (1%)
    all_to_all x1, blocking collectives, local_step(): recv_buf = lax.all_to_all(send_buf, 'ep', 1, 1, tiled=True)  72.3 us
    all_to_all x1, waiting for transfers between devices, local_step(): lax.all_to_all(expert_out.reshape(local_count, group_size, capacity, hidd...  41.9 us
    add x1, other arithmetic, route_layout(): (sorted_expert % local_count * group_size + sorted_expert // local_count)...  35.7 us
    dot_general x1, matrix products, expert_swiglu(): jnp.einsum('eci,eih->ech', activated, w_down, preferred_element_type=jnp....  28.6 us
    reshape x2, local copies, waits for them, and re-layouts, local_step(): normed_pad[slot_token]  15.3 us
    gather x5, local copies, waits for them, and re-layouts, route_weights(): jnp.take_along_axis(jax.nn.softmax(logits, axis=-1), topk_idx, axis=1)  13.2 us
    gather x1, local copies, waits for them, and re-layouts, local_step(): back_buf.reshape(local_count * group_size * capacity, hidden_size)[row_slot]  12.4 us
    dot_general x1, matrix products, expert_swiglu(): jnp.einsum('ech,ehi->eci', expert_in, w_up, preferred_element_type=jnp.fl...  12 us
  transfers between devices with their start and end apart: 1, of which 1 were waited for; matrix products, arithmetic and copies ran while one was open for 7% of the time, Pallas kernels for 0%

commit v1 on v0

v1 whole, which is shorter than its diff:
```python
import functools

import jax
import jax.numpy as jnp
from jax import lax
from jax.experimental import pallas as pl
from jax.experimental.pallas import tpu as pltpu
from jax.sharding import PartitionSpec as P

NORM_EPS = 1e-6
MESH = pl.DeviceIdType.MESH
F32 = jnp.float32
BF16 = jnp.bfloat16

OWN, XN, YN, DG = 0, 1, 2, 3
SS_SLOT = {XN: 0, YN: 1, DG: 0, OWN: 1}
PEERS = [(q, r) for q in range(4) for r in range(2) if (q, r) != (0, 0)]


def dot(a, b):
    return jnp.dot(a, b, preferred_element_type=F32)


def moe_kernel(cfg, hid, gain, rw, topk, wg, wu, wd, sg, su, sd, out,
               gu, dn, g, rwp, wloc, win, rankm, x, act, o, comb, ash, acc, ss, sr, s, rx, ry, qx, qy,
               gu_sem, dn_sem, ag_s, ag_r, sib_s, sib_r, ici_s, ici_r):
    T, H, FF, EL, SLOT, NB, BW = cfg
    HT = T // 2
    me = lax.axis_index("ep")
    core, xx, yy = me % 2, (me // 2) % 2, me // 4

    def ep_of(q, r):
        nx = 1 - xx if q % 2 else xx
        ny = 1 - yy if q // 2 else yy
        nc = 1 - core if r else core
        return 4 * ny + 2 * nx + nc

    def rcopy(src, dst, send, recv, q, r):
        return pltpu.make_async_remote_copy(src_ref=src, dst_ref=dst, send_sem=send, recv_sem=recv,
                                            device_id={"ep": ep_of(q, r)}, device_id_type=MESH)

    lo, hi = pl.ds(0, HT), pl.ds(HT, HT)
    ag = {
        0: (g.at[OWN, 0], g.at[OWN, 1], OWN, 1),
        1: (g.at[OWN, 0, lo], g.at[XN, 0, lo], XN, 0),
        2: (g.at[OWN, 0, hi], g.at[YN, 0, hi], YN, 0),
        3: (g.at[OWN, 0, hi], g.at[XN, 0, hi], XN, 0),
        4: (g.at[OWN, 0, lo], g.at[YN, 0, lo], YN, 0),
        5: (g.at[XN, 0, lo], g.at[DG, 0, lo], YN, 0),
        6: (g.at[YN, 0, hi], g.at[DG, 0, hi], XN, 0),
        7: (g.at[XN, 0, lo], g.at[XN, 1, lo], OWN, 1),
        8: (g.at[YN, 0, hi], g.at[YN, 1, hi], OWN, 1),
        9: (g.at[XN, 0, hi], g.at[XN, 1, hi], OWN, 1),
        10: (g.at[YN, 0, lo], g.at[YN, 1, lo], OWN, 1),
        11: (g.at[DG, 0, lo], g.at[DG, 1, lo], OWN, 1),
        12: (g.at[DG, 0, hi], g.at[DG, 1, hi], OWN, 1),
    }
    for j, (q, r) in enumerate(PEERS):
        ag[13 + j] = (wloc.at[ep_of(q, r)], win.at[q, r], q, r)

    def agc(k):
        src, dst, q, r = ag[k]
        return rcopy(src, dst, ag_s.at[k], ag_r.at[k], q, r)

    def sibc(q, n):
        return rcopy(ss.at[SS_SLOT[q], n], sr.at[q, n], sib_s.at[q, n], sib_r.at[q, n], OWN, 1)

    def icic(k, n):
        src, dst, q = [
            (s.at[XN - 1, n, lo], rx.at[n, lo], XN),
            (s.at[YN - 1, n, hi], ry.at[n, hi], YN),
            (s.at[DG - 1, n, lo], qx.at[n], XN),
            (s.at[DG - 1, n, hi], qy.at[n], YN),
            (s.at[YN - 1, n, lo], ry.at[n, lo], YN),
            (s.at[XN - 1, n, hi], rx.at[n, hi], XN),
        ][k]
        return rcopy(src, dst, ici_s.at[k, n], ici_r.at[k, n], q, 0)

    def gu_loads(e, slot):
        return [pltpu.make_async_copy(wg.at[e], gu.at[slot, :, pl.ds(0, FF)], gu_sem.at[slot, 0]),
                pltpu.make_async_copy(wu.at[e], gu.at[slot, :, pl.ds(FF, FF)], gu_sem.at[slot, 1])]

    def dn_load(n, slot):
        return pltpu.make_async_copy(wd.at[:, :, pl.ds(pl.multiple_of(n * BW, BW), BW)], dn.at[slot], dn_sem.at[slot])

    def sd_load(n, slot):
        return pltpu.make_async_copy(sd.at[:, :, pl.ds(pl.multiple_of(n * BW, BW), BW)], dn.at[slot, pl.ds(0, 2)],
                                     dn_sem.at[slot])

    sg_load = pltpu.make_async_copy(sg, gu.at[2], gu_sem.at[2, 0])
    su_load = pltpu.make_async_copy(su, gu.at[3], gu_sem.at[3, 0])
    sg_load.start()
    su_load.start()
    sd_load(0, 0).start()
    sd_load(1, 1).start()
    for e in range(2):
        for c in gu_loads(e, e):
            c.start()

    barrier = pltpu.get_barrier_semaphore()
    for q, r in PEERS:
        pl.semaphore_signal(barrier, inc=1, device_id={"ep": ep_of(q, r)}, device_id_type=MESH)

    h = hid[...].astype(F32)
    inv = lax.rsqrt(jnp.mean(h * h, axis=-1, keepdims=True) + NORM_EPS)
    g[OWN, 0] = (h * inv * gain[...]).astype(BF16)
    pl.semaphore_wait(barrier, len(PEERS))
    for k in (1, 2, 0, 3, 4):
        agc(k).start()

    rwp[...] = jnp.zeros_like(rwp)
    rwp[:, 0:64] = rw[...]
    logits = dot(g[OWN, 0], rwp[...])
    lane = lax.broadcasted_iota(jnp.int32, logits.shape, 1)
    logits = jnp.where(lane < 64, logits, -jnp.inf)
    ex = jnp.exp(logits - jnp.max(logits, axis=-1, keepdims=True))
    p = ex / jnp.sum(ex, axis=-1, keepdims=True)
    chosen = topk[:, 0:1] == lane
    for j in range(1, topk.shape[1]):
        chosen = jnp.logical_or(chosen, topk[:, j:j + 1] == lane)
    wt = jnp.where(chosen, p, -1.0).T
    wloc[...] = wt[0:64].reshape(8, EL, T)
    for j in range(len(PEERS)):
        agc(13 + j).start()
    win[OWN, 0] = wloc[me]

    sg_load.wait()
    su_load.wait()

    @pl.loop(0, ash.shape[1] // BW)
    def _(n):
        cols = pl.ds(pl.multiple_of(n * BW, BW), BW)
        ga = dot(g[OWN, 0], gu[2, :, cols])
        up = dot(g[OWN, 0], gu[3, :, cols])
        ash[:, cols] = (jax.nn.silu(ga) * up).astype(BF16)

    for e in (2, 3):
        for c in gu_loads(e, e):
            c.start()

    agc(1).wait_recv()
    agc(5).start()
    agc(7).start()
    agc(2).wait_recv()
    agc(6).start()
    agc(8).start()

    @pl.loop(0, NB)
    def _(n):
        cols = pl.ds(pl.multiple_of(n * BW, BW), BW)
        slot = n % 2
        sd_load(n, slot).wait()
        acc[n] = hid[:, cols].astype(F32) + dot(ash[...], dn[slot, 0:2].reshape(2 * FF, BW))

        @pl.when(n + 2 < NB)
        def _():
            sd_load(n + 2, slot).start()

        @pl.when(n + 2 >= NB)
        def _():
            dn_load(n + 2 - NB, slot).start()

    for j in range(len(PEERS)):
        agc(13 + j).wait_recv()
    wall = win[...].reshape(8 * EL, T)
    upper = (lax.broadcasted_iota(jnp.int32, (T, T), 0) < lax.broadcasted_iota(jnp.int32, (T, T), 1))
    upper = jnp.where(upper, 1.0, 0.0).astype(BF16)
    rank = dot(jnp.where(wall >= 0, 1.0, 0.0).astype(BF16), upper)
    rankm[...] = jnp.where(wall >= 0, rank, -1.0).reshape(4, 2, EL, T)

    def dispatch(q, r, i):
        rk = rankm[q, r]
        w = win[q, r]
        slot_id = lax.broadcasted_iota(jnp.int32, (EL, SLOT, T), 1).astype(F32)
        hit = jnp.broadcast_to(rk[:, None, :], (EL, SLOT, T)) == slot_id
        pick = jnp.where(hit, 1.0, 0.0).reshape(EL * SLOT, T).astype(BF16)
        x[:, i] = dot(pick, g[q, r]).astype(BF16).reshape(EL, SLOT, H)
        cw = jnp.where(hit, jnp.broadcast_to(w[:, None, :], (EL, SLOT, T)), 0.0).reshape(EL * SLOT, T).T
        c1 = cw.astype(BF16)
        rest = cw - c1.astype(F32)
        c2 = rest.astype(BF16)
        comb[i, 0] = c1
        comb[i, 1] = c2
        comb[i, 2] = (rest - c2.astype(F32)).astype(BF16)

    def finish(q, n):
        sibc(q, n).wait_recv()
        if q == OWN:
            acc[n] = acc[n] + sr[q, n]
            return
        s[q - 1, n] = s[q - 1, n] + sr[q, n]
        if q == XN:
            icic(0, n).start()
        elif q == YN:
            icic(1, n).start()
        else:
            icic(2, n).start()
            icic(3, n).start()

    def relay(n):
        icic(2, n).wait_recv()
        s[YN - 1, n, lo] = s[YN - 1, n, lo] + qx[n]
        icic(4, n).start()
        icic(3, n).wait_recv()
        s[XN - 1, n, hi] = s[XN - 1, n, hi] + qy[n]
        icic(5, n).start()

    def expert_pass(p, chips, down_first, between, mid_steps):
        owners = 2 * len(chips)
        rows = owners * SLOT

        @pl.loop(0, owners)
        def _(i):
            dispatch(chips[0] + i // 2, i % 2, i)

        @pl.loop(0, EL)
        def _(i):
            e = EL - 1 - i if p == 1 else i
            slot = e % 4
            fresh = (e >= 0) if p == 0 else ((e < 4) if p == 1 else (e >= 4))

            @pl.when(fresh)
            def _():
                for c in gu_loads(e, slot):
                    c.wait()

            xe = x[e, 0:owners].reshape(rows, H)
            gua = dot(xe, gu[slot])
            act[e, 0:rows] = (jax.nn.silu(gua[:, 0:FF]) * gua[:, FF:2 * FF]).astype(BF16)

            @pl.when(i < 4)
            def _():
                nxt = e - 4 if p == 1 else e + 4
                for c in gu_loads(nxt, slot):
                    c.start()

            mid_steps(i)

        between()

        @pl.loop(0, NB)
        def _(n):
            slot = (n + NB * (p + 1)) % 2
            dn_load(n, slot).wait()
            for e in range(EL):
                res = dot(act[e, 0:rows], dn[slot, e]).astype(BF16)
                o[0:owners, e] = res.reshape(owners, SLOT, BW)

            @pl.when(jnp.logical_or(n + 2 < NB, p < 2))
            def _():
                dn_load((n + 2) % NB, slot).start()

            for i in sorted(range(owners), key=lambda i: -(i % 2)):
                q = chips[i // 2]
                oo = o[i].reshape(EL * SLOT, BW)
                part = dot(comb[i, 0], oo) + dot(comb[i, 1], oo) + dot(comb[i, 2], oo)
                if i % 2:
                    if p == 1:
                        sibc(XN, n).wait_send()
                    elif p == 2:
                        sibc(YN, n).wait_send()
                    ss[SS_SLOT[q], n] = part
                    sibc(q, n).start()
                elif q == OWN:
                    acc[n] = acc[n] + part
                else:
                    s[q - 1, n] = part

            @pl.when(n > 0)
            def _():
                for q in chips:
                    finish(q, n - 1)

            down_first(n)

        for q in chips:
            finish(q, NB - 1)

    nothing = lambda *a: None

    agc(3).wait_recv()
    agc(9).start()
    agc(4).wait_recv()
    agc(10).start()
    for k in (7, 8, 9, 10):
        agc(k).wait_recv()

    def forward_diag():
        agc(5).wait_recv()
        agc(11).start()
        agc(6).wait_recv()
        agc(12).start()

    expert_pass(0, [XN, YN], nothing, forward_diag, nothing)

    agc(11).wait_recv()
    agc(12).wait_recv()
    expert_pass(1, [DG], nothing, nothing, nothing)

    agc(0).wait_recv()

    def relay_gu(i):
        @pl.when(i % 3 == 1)
        def _():
            relay(i // 3)

    def relay_dn(n):
        @pl.when(n == 1)
        def _():
            relay(3)

        @pl.when(n == 4)
        def _():
            relay(4)

    expert_pass(2, [OWN], relay_dn, nothing, relay_gu)

    for n in range(NB):
        for k in (0, 5, 1, 4):
            icic(k, n).wait_recv()
        out[:, n * BW:(n + 1) * BW] = (acc[n] + rx[n] + ry[n]).astype(BF16)

    for k in range(13 + len(PEERS)):
        agc(k).wait_send()
    for n in range(NB):
        for q in (DG, OWN):
            sibc(q, n).wait_send()
        for k in range(6):
            icic(k, n).wait_send()


def solution(mesh):
    def local_step(hidden, norm_gain, router_w, topk_idx, w_gate, w_up, w_down, shared_gate, shared_up, shared_down):
        T, H = hidden.shape
        EL, _, FF = w_gate.shape
        BW = 256
        NB = H // BW
        SLOT = 48
        cfg = (T, H, FF, EL, SLOT, NB, BW)
        vm = pl.BlockSpec(memory_space=pltpu.VMEM)
        anym = pl.BlockSpec(memory_space=pl.ANY)
        dma = pltpu.SemaphoreType.DMA
        n_ag = 13 + len(PEERS)
        return pl.pallas_call(
            functools.partial(moe_kernel, cfg),
            out_shape=jax.ShapeDtypeStruct((T, H), BF16),
            in_specs=[vm, vm, vm, vm] + [anym] * 6,
            out_specs=vm,
            scratch_shapes=[
                pltpu.VMEM((4, H, 2 * FF), BF16),
                pltpu.VMEM((2, EL, FF, BW), BF16),
                pltpu.VMEM((4, 2, T, H), BF16),
                pltpu.VMEM((H, 128), BF16),
                pltpu.VMEM((8, EL, T), F32),
                pltpu.VMEM((4, 2, EL, T), F32),
                pltpu.VMEM((4, 2, EL, T), F32),
                pltpu.VMEM((EL, 4, SLOT, H), BF16),
                pltpu.VMEM((EL, 4 * SLOT, FF), BF16),
                pltpu.VMEM((4, EL, SLOT, BW), BF16),
                pltpu.VMEM((4, 3, T, EL * SLOT), BF16),
                pltpu.VMEM((T, 2 * FF), BF16),
                pltpu.VMEM((NB, T, BW), F32),
                pltpu.VMEM((2, NB, T, BW), F32),
                pltpu.VMEM((4, NB, T, BW), F32),
                pltpu.VMEM((3, NB, T, BW), F32),
                pltpu.VMEM((NB, T, BW), F32),
                pltpu.VMEM((NB, T, BW), F32),
                pltpu.VMEM((NB, T // 2, BW), F32),
                pltpu.VMEM((NB, T // 2, BW), F32),
                dma((4, 2)), dma((2,)),
                dma((n_ag,)), dma((n_ag,)), dma((4, NB)), dma((4, NB)), dma((6, NB)), dma((6, NB)),
            ],
            compiler_params=pltpu.CompilerParams(collective_id=0, has_side_effects=True, vmem_limit_bytes=67043328),
            name="moe_block",
        )(hidden, norm_gain.reshape(1, H), router_w, topk_idx, w_gate, w_up, w_down, shared_gate, shared_up,
          shared_down.reshape(2, FF, H))

    token_spec = P(('dp', 'ep'), None)
    expert_spec = P('ep', None, None)
    return jax.shard_map(
        local_step,
        mesh=mesh,
        in_specs=(token_spec, P(None), P(None, None), token_spec, expert_spec, expert_spec, expert_spec,
                  P(None, None), P(None, None), P(None, None)),
        out_specs=token_spec,
        check_vma=False,
    )
```

time: 349 us -> 100 us (0.29)
  local copies, waits for them, and re-layouts: 109 us -> 6.54 us
  Pallas kernels: 0 us -> 93.5 us
  blocking collectives: 72.3 us -> 0 us
  other arithmetic: 65.4 us -> 0 us
  matrix products: 53.8 us -> 0 us
  waiting for transfers between devices: 41.9 us -> 0 us
  starting transfers between devices: 4.86 us -> 0 us
    pallas_call x0 -> x1, Pallas kernels: none -> 93.5 us  [local_step(): pl.pallas_call(functools.partial(moe_kernel, cfg), out_shape=jax.ShapeDty...]
    all_to_all x1 -> x0, blocking collectives: 72.3 us -> none  [local_step(): recv_buf = lax.all_to_all(send_buf, 'ep', 1, 1, tiled=True)]
    dot_general x5 -> x0, matrix products: 53.8 us -> none  [the longest x1 28.6 us: expert_swiglu(): jnp.einsum('eci,eih->ech', activated, w_down, preferred_element_type=jnp....]
    gather x12 -> x0, local copies, waits for them, and re-layouts: 45.4 us -> none  [the longest x5 13.2 us: route_weights(): jnp.take_along_axis(jax.nn.softmax(logits, axis=-1), topk_idx, axis=1)]
    all_to_all x1 -> x0, waiting for transfers between devices: 41.9 us -> none  [local_step(): lax.all_to_all(expert_out.reshape(local_count, group_size, capacity, hidd...]
    add x1 -> x0, other arithmetic: 35.7 us -> none  [route_layout(): (sorted_expert % local_count * group_size + sorted_expert // local_count)...]
    reshape x5 -> x1, local copies, waits for them, and re-layouts: 24.8 us -> 1.29 us  [local_step(): norm_gain.reshape(1, H)]
    convert_element_type x2 -> x0, local copies, waits for them, and re-layouts: 16.2 us -> none  [the longest x1 8.44 us: expert_swiglu(): jnp.einsum('eci,eih->ech', activated, w_down, preferred_element_type=jnp....]
  transfers between devices with their start and end apart: 1 -> 0, of which waited for: 1 -> 0; matrix products, arithmetic and copies ran while one was open for 7% -> 0% of each run, Pallas kernels for 0% -> 0%
where the time goes in v1:
time: 100 us
  Pallas kernels  93.5 us (94%)
  local copies, waits for them, and re-layouts  6.54 us (7%)
    pallas_call x1, Pallas kernels, local_step(): pl.pallas_call(functools.partial(moe_kernel, cfg), out_shape=jax.ShapeDty...  93.5 us
    unnamed x3, local copies, waits for them, and re-layouts  5.25 us

profile of v1, /device:TPU:0, one launch (start us, length us, event | category | flops | bytes accessed | tf_op | source)
XLA Modules:
  0.0 100.1 jit_solution(13096214777784805274)
XLA Ops:
  0.0 1.3 %reshape.6.gain = f32[1,1280]{1,0:T(1,128)} reshape(f32[1280]{0:T(1024)} %param.11) | data formatting | bytes 10240 | tf_op jit(solution)/shard_map/reshape | solution.py:375
  1.3 1.5 %copy.12.topk = s32[256,6]{1,0:T(8,128)} copy(s32[256,6]{0,1:T(8,128)} %param.13) | data formatting | bytes 12288 | tf_op args[3]
  2.8 1.8 %copy.11.rw = bf16[1280,64]{1,0:T(8,128)(2,1)} copy(bf16[1280,64]{0,1:T(8,128)(2,1)} %param.12) | data formatting | bytes 327680 | tf_op args[2]
  4.6 93.5 %moe_block.1 = bf16[256,1280]{1,0:T(8,128)(2,1)} custom-call(bf16[256,1280]{1,0:T(8,128)(2,1)} %hid.1, f32[1,1280]{1,0:T(1,128)} %reshape.6.gain, bf16[1280,64]{1,0:T(8,128)(2,1)} %copy.11.rw, s32[256,6]{1,0:T(8,128)} %copy.12.topk, bf16[8,1280,896]{2,1,0:T(8,128)(2,1)} %wg.1, bf16[8,1280,896]{2,1,0:T(8,128)(2,1)} %wu.1, bf16[8,896,1280]{2,1,0:T(8,128)(2,1)} %wd.1, ...), custom_call_target="tpu_custom_call" | custom-call | tf_op jit(solution)/shard_map/moe_block/pallas_call | solution.py:344
  98.1 2.0 %copy.14 = bf16[256,1280]{1,0:T(8,128)(2,1)} copy(bf16[256,1280]{1,0:T(8,128)(2,1)} %moe_block.1) | data formatting | bytes 1310720

commit v2 on v1

v2 whole, which is shorter than its diff:
```python
import functools

import jax
import jax.numpy as jnp
from jax import lax
from jax.experimental import pallas as pl
from jax.experimental.pallas import tpu as pltpu
from jax.sharding import PartitionSpec as P

NORM_EPS = 1e-6
MESH = pl.DeviceIdType.MESH
F32 = jnp.float32
BF16 = jnp.bfloat16

OWN, XN, YN, DG = 0, 1, 2, 3
SR_SLOT = {XN: 0, YN: 1, DG: 2, OWN: 0}
SS_SLOT = {XN: 0, YN: 1, DG: 0, OWN: 1}
NAG = 10
PEERS = [(q, r) for q in range(4) for r in range(2) if (q, r) != (0, 0)]


def dot(a, b):
    return jnp.dot(a, b, preferred_element_type=F32)


def moe_kernel(cfg, hid, gain, rwt, topkt, wg, wu, wd, sg, su, sd, out,
               gu, dn, g, wloc, win, rankm, x, act, o, comb, ash, acc, ss, sr, s, rx, ry, qx, qy,
               gu_sem, dn_sem, ag_s, ag_r, sib_s, sib_r, ici_s, ici_r):
    T, H, FF, EL, SLOT, NB, BW, NS = cfg
    HT = T // 2
    me = lax.axis_index("ep")
    core, xx, yy = me % 2, (me // 2) % 2, me // 4

    def ep_of(q, r):
        return 4 * ((yy + q // 2) % 2) + 2 * ((xx + q % 2) % 2) + (core + r) % 2

    def rcopy(src, dst, send, recv, q, r):
        return pltpu.make_async_remote_copy(src_ref=src, dst_ref=dst, send_sem=send, recv_sem=recv,
                                            device_id={"ep": ep_of(q, r)}, device_id_type=MESH)

    lo, hi = pl.ds(0, HT), pl.ds(HT, HT)
    qa, qb = 1 + core, 2 - core
    ha = pl.ds(pl.multiple_of(core * HT, HT), HT)
    hb = pl.ds(pl.multiple_of((1 - core) * HT, HT), HT)
    ag = {
        0: (g.at[OWN, 0], g.at[OWN, 1], OWN, 1),
        1: (g.at[OWN, 0, lo], g.at[qa, 0, lo], qa, 0),
        2: (g.at[OWN, 0, hi], g.at[qa, 0, hi], qa, 0),
        3: (g.at[OWN, 0], g.at[qb, 0], qb, 0),
        4: (g.at[qa, 0, ha], g.at[DG, 0, ha], qb, 0),
        5: (g.at[qb, 0, hb], g.at[DG, 0, hb], qa, 0),
        6: (g.at[qa, 0], g.at[qa, 1], OWN, 1),
        7: (g.at[qb, 0], g.at[qb, 1], OWN, 1),
        8: (g.at[DG, 0, ha], g.at[DG, 1, ha], OWN, 1),
        9: (g.at[DG, 0, hb], g.at[DG, 1, hb], OWN, 1),
    }
    for j, (q, r) in enumerate(PEERS):
        ag[NAG + j] = (wloc.at[ep_of(q, r)], win.at[q, r], q, r)

    def agc(k):
        src, dst, q, r = ag[k]
        return rcopy(src, dst, ag_s.at[k], ag_r.at[k], q, r)

    def sibc(q, n):
        return rcopy(ss.at[SS_SLOT[q], n], sr.at[SR_SLOT[q], n], sib_s.at[q, n], sib_r.at[q, n], OWN, 1)

    def icic(k, n):
        src, dst, q = [
            (s.at[XN - 1, n, lo], rx.at[n, lo], XN),
            (s.at[YN - 1, n, hi], ry.at[n, hi], YN),
            (s.at[DG - 1, n, lo], qx.at[n], XN),
            (s.at[DG - 1, n, hi], qy.at[n], YN),
            (s.at[YN - 1, n, lo], ry.at[n, lo], YN),
            (s.at[XN - 1, n, hi], rx.at[n, hi], XN),
        ][k]
        return rcopy(src, dst, ici_s.at[k, n], ici_r.at[k, n], q, 0)

    def gu_loads(e, slot):
        return [pltpu.make_async_copy(wg.at[e], gu.at[slot, :, pl.ds(0, FF)], gu_sem.at[slot, 0]),
                pltpu.make_async_copy(wu.at[e], gu.at[slot, :, pl.ds(FF, FF)], gu_sem.at[slot, 1])]

    def dn_load(n, slot):
        return pltpu.make_async_copy(wd.at[:, :, pl.ds(pl.multiple_of(n * BW, BW), BW)], dn.at[slot], dn_sem.at[slot])

    def sd_load(n, slot):
        return pltpu.make_async_copy(sd.at[:, :, pl.ds(pl.multiple_of(n * BW, BW), BW)], dn.at[slot, pl.ds(0, 2)],
                                     dn_sem.at[slot])

    sg_load = pltpu.make_async_copy(sg, gu.at[NS - 2], gu_sem.at[NS - 2, 0])
    su_load = pltpu.make_async_copy(su, gu.at[NS - 1], gu_sem.at[NS - 1, 0])
    sg_load.start()
    su_load.start()
    sd_load(0, 0).start()
    sd_load(1, 1).start()
    for e in range(NS - 2):
        for c in gu_loads(e, e):
            c.start()

    barrier = pltpu.get_barrier_semaphore()
    for q, r in PEERS:
        pl.semaphore_signal(barrier, inc=1, device_id={"ep": ep_of(q, r)}, device_id_type=MESH)

    h = hid[...].astype(F32)
    inv = lax.rsqrt(jnp.mean(h * h, axis=-1, keepdims=True) + NORM_EPS)
    g[OWN, 0] = (h * inv * gain[...][None, :]).astype(BF16)
    pl.semaphore_wait(barrier, len(PEERS))
    agc(1).start()
    agc(0).start()

    logits = lax.dot_general(rwt[...], g[OWN, 0], (((1,), (1,)), ((), ())), preferred_element_type=F32)
    ex = jnp.exp(logits - jnp.max(logits, axis=0, keepdims=True))
    p = ex / jnp.sum(ex, axis=0, keepdims=True)
    expert = lax.broadcasted_iota(jnp.int32, logits.shape, 0)
    chosen = topkt[0:1, :] == expert
    for j in range(1, topkt.shape[0]):
        chosen = jnp.logical_or(chosen, topkt[j:j + 1, :] == expert)
    wloc[...] = jnp.where(chosen, p, -1.0).reshape(8, EL, T)
    for j in range(len(PEERS)):
        agc(NAG + j).start()
    agc(2).start()
    win[OWN, 0] = wloc[me]

    sg_load.wait()
    su_load.wait()

    @pl.loop(0, ash.shape[1] // BW)
    def _(n):
        cols = pl.ds(pl.multiple_of(n * BW, BW), BW)
        ga = dot(g[OWN, 0], gu[NS - 2, :, cols])
        up = dot(g[OWN, 0], gu[NS - 1, :, cols])
        ash[:, cols] = (jax.nn.silu(ga) * up).astype(BF16)

    for e in (NS - 2, NS - 1):
        for c in gu_loads(e, e):
            c.start()

    @pl.loop(0, NB)
    def _(n):
        cols = pl.ds(pl.multiple_of(n * BW, BW), BW)
        slot = n % 2
        sd_load(n, slot).wait()
        acc[n] = hid[:, cols].astype(F32) + dot(ash[...], dn[slot, 0:2].reshape(2 * FF, BW))

        @pl.when(n + 2 < NB)
        def _():
            sd_load(n + 2, slot).start()

        @pl.when(n + 2 >= NB)
        def _():
            dn_load(n + 2 - NB, slot).start()

    agc(1).wait_send()
    agc(2).wait_send()
    agc(3).start()
    agc(1).wait_recv()
    agc(2).wait_recv()
    agc(6).start()
    agc(4).start()

    for j in range(len(PEERS)):
        agc(NAG + j).wait_recv()
    wall = win[...].reshape(8 * EL, T)
    upper = (lax.broadcasted_iota(jnp.int32, (T, T), 0) < lax.broadcasted_iota(jnp.int32, (T, T), 1))
    upper = jnp.where(upper, 1.0, 0.0).astype(BF16)
    rank = dot(jnp.where(wall >= 0, 1.0, 0.0).astype(BF16), upper)
    rankm[...] = jnp.where(wall >= 0, rank, -1.0).reshape(4, 2, EL, T)

    def hits(q, r):
        slot_id = lax.broadcasted_iota(jnp.int32, (EL, SLOT, T), 1).astype(F32)
        return jnp.broadcast_to(rankm[q, r][:, None, :], (EL, SLOT, T)) == slot_id

    def dispatch(q, r, i):
        pick = jnp.where(hits(q, r), 1.0, 0.0).reshape(EL * SLOT, T).astype(BF16)
        x[:, i] = dot(pick, g[q, r]).astype(BF16).reshape(EL, SLOT, H)

    def build_comb(q, r, i):
        w = jnp.broadcast_to(win[q, r][:, None, :], (EL, SLOT, T))
        cw = jnp.where(hits(q, r), w, 0.0).reshape(EL * SLOT, T).T
        c1 = cw.astype(BF16)
        rest = cw - c1.astype(F32)
        c2 = rest.astype(BF16)
        comb[i, 0] = c1
        comb[i, 1] = c2
        comb[i, 2] = (rest - c2.astype(F32)).astype(BF16)

    def finish(q, n):
        sibc(q, n).wait_recv()
        if q == OWN:
            acc[n] = acc[n] + sr[SR_SLOT[q], n]
            return
        s[q - 1, n] = s[q - 1, n] + sr[SR_SLOT[q], n]
        if q == XN:
            icic(0, n).start()
        elif q == YN:
            icic(1, n).start()
        else:
            icic(2, n).start()
            icic(3, n).start()

    def relay(n):
        icic(2, n).wait_recv()
        s[YN - 1, n, lo] = s[YN - 1, n, lo] + qx[n]
        icic(4, n).start()
        icic(3, n).wait_recv()
        s[XN - 1, n, hi] = s[XN - 1, n, hi] + qy[n]
        icic(5, n).start()

    def gate_up(p, a0, a1, step):
        @pl.loop(0, EL)
        def _(i):
            e = EL - 1 - i if p % 2 else i
            slot = e % NS

            @pl.when(i >= (NS if p else 0))
            def _():
                for c in gu_loads(e, slot):
                    c.wait()

            gua = dot(x[e].reshape(2 * SLOT, H), gu[slot])
            res = (jax.nn.silu(gua[:, 0:FF]) * gua[:, FF:2 * FF]).astype(BF16)
            act[e, a0] = res[0:SLOT]
            act[e, a1] = res[SLOT:2 * SLOT]

            @pl.when(i < EL - NS)
            def _():
                for c in gu_loads(e - NS if p % 2 else e + NS, slot):
                    c.start()

            step(i)

    def down(p, chips, step):
        owners = 2 * len(chips)

        @pl.loop(0, NB)
        def _(n):
            slot = (n + NB * (p + 1)) % 2
            dn_load(n, slot).wait()
            for e in range(EL):
                res = dot(act[e, 0:owners].reshape(owners * SLOT, FF), dn[slot, e]).astype(BF16)
                o[0:owners, e] = res.reshape(owners, SLOT, BW)

            @pl.when(jnp.logical_or(n + 2 < NB, p < 2))
            def _():
                dn_load((n + 2) % NB, slot).start()

            for i in sorted(range(owners), key=lambda i: -(i % 2)):
                q = chips[i // 2]
                oo = o[i].reshape(EL * SLOT, BW)
                part = dot(comb[i, 0], oo) + dot(comb[i, 1], oo) + dot(comb[i, 2], oo)
                if i % 2:
                    if p:
                        sibc(XN if p == 1 else YN, n).wait_send()
                    ss[SS_SLOT[q], n] = part
                    sibc(q, n).start()
                elif q == OWN:
                    acc[n] = acc[n] + part
                else:
                    s[q - 1, n] = part

            @pl.when(n > 0)
            def _():
                for q in chips:
                    finish(q, n - 1)

            step(n)

        for q in chips:
            finish(q, NB - 1)

    nothing = lambda i: None

    @pl.loop(0, 4)
    def _(i):
        build_comb(1 + i // 2, i % 2, i)

    def second_arrival(i):
        @pl.when(i == 6)
        def _():
            agc(3).wait_recv()
            agc(7).start()
            agc(5).start()

    agc(6).wait_recv()
    dispatch(qa, 0, 0)
    dispatch(qb, 1, 1)
    gate_up(0, 2 * (qa - 1), 2 * (qb - 1) + 1, second_arrival)
    agc(7).wait_recv()
    dispatch(qb, 0, 0)
    dispatch(qa, 1, 1)
    gate_up(1, 2 * (qb - 1), 2 * (qa - 1) + 1, nothing)
    agc(4).wait_recv()
    agc(8).start()
    agc(5).wait_recv()
    agc(9).start()
    down(0, [XN, YN], nothing)

    for r in range(2):
        build_comb(DG, r, r)
    agc(8).wait_recv()
    agc(9).wait_recv()
    for r in range(2):
        dispatch(DG, r, r)
    gate_up(2, 0, 1, nothing)
    down(1, [DG], nothing)

    def relay_gu(i):
        @pl.when(i % 3 == 1)
        def _():
            relay(i // 3)

    def relay_dn(n):
        @pl.when(n == 1)
        def _():
            relay(3)

        @pl.when(n == 4)
        def _():
            relay(4)

    agc(0).wait_recv()
    for r in range(2):
        build_comb(OWN, r, r)
        dispatch(OWN, r, r)
    gate_up(3, 0, 1, relay_gu)
    down(2, [OWN], relay_dn)

    for n in range(NB):
        for k in (0, 5, 1, 4):
            icic(k, n).wait_recv()
        out[:, n * BW:(n + 1) * BW] = (acc[n] + rx[n] + ry[n]).astype(BF16)

    for k in range(NAG + len(PEERS)):
        if k not in (1, 2):
            agc(k).wait_send()
    for n in range(NB):
        for q in (DG, OWN):
            sibc(q, n).wait_send()
        for k in range(6):
            icic(k, n).wait_send()


def solution(mesh):
    def local_step(hidden, norm_gain, router_w, topk_idx, w_gate, w_up, w_down, shared_gate, shared_up, shared_down):
        T, H = hidden.shape
        EL, _, FF = w_gate.shape
        BW = 256
        NB = H // BW
        SLOT = 48
        NS = 5
        cfg = (T, H, FF, EL, SLOT, NB, BW, NS)
        vm = pl.BlockSpec(memory_space=pltpu.VMEM)
        anym = pl.BlockSpec(memory_space=pl.ANY)
        dma = pltpu.SemaphoreType.DMA
        n_ag = NAG + len(PEERS)
        return pl.pallas_call(
            functools.partial(moe_kernel, cfg),
            out_shape=jax.ShapeDtypeStruct((T, H), BF16),
            in_specs=[vm, vm, vm, vm] + [anym] * 6,
            out_specs=vm,
            scratch_shapes=[
                pltpu.VMEM((NS, H, 2 * FF), BF16),
                pltpu.VMEM((2, EL, FF, BW), BF16),
                pltpu.VMEM((4, 2, T, H), BF16),
                pltpu.VMEM((8, EL, T), F32),
                pltpu.VMEM((4, 2, EL, T), F32),
                pltpu.VMEM((4, 2, EL, T), F32),
                pltpu.VMEM((EL, 2, SLOT, H), BF16),
                pltpu.VMEM((EL, 4, SLOT, FF), BF16),
                pltpu.VMEM((4, EL, SLOT, BW), BF16),
                pltpu.VMEM((4, 3, T, EL * SLOT), BF16),
                pltpu.VMEM((T, 2 * FF), BF16),
                pltpu.VMEM((NB, T, BW), F32),
                pltpu.VMEM((2, NB, T, BW), F32),
                pltpu.VMEM((3, NB, T, BW), F32),
                pltpu.VMEM((3, NB, T, BW), F32),
                pltpu.VMEM((NB, T, BW), F32),
                pltpu.VMEM((NB, T, BW), F32),
                pltpu.VMEM((NB, T // 2, BW), F32),
                pltpu.VMEM((NB, T // 2, BW), F32),
                dma((NS, 2)), dma((2,)),
                dma((n_ag,)), dma((n_ag,)), dma((4, NB)), dma((4, NB)), dma((6, NB)), dma((6, NB)),
            ],
            compiler_params=pltpu.CompilerParams(collective_id=0, has_side_effects=True, vmem_limit_bytes=67043328),
            name="moe_block",
        )(hidden, norm_gain, router_w.T, topk_idx.T, w_gate, w_up, w_down, shared_gate, shared_up,
          shared_down.reshape(2, FF, H))

    token_spec = P(('dp', 'ep'), None)
    expert_spec = P('ep', None, None)
    return jax.shard_map(
        local_step,
        mesh=mesh,
        in_specs=(token_spec, P(None), P(None, None), token_spec, expert_spec, expert_spec, expert_spec,
                  P(None, None), P(None, None), P(None, None)),
        out_specs=token_spec,
        check_vma=False,
    )
```

time: 100 us -> 95 us (0.950)
  local copies, waits for them, and re-layouts: 6.54 us -> 1.97 us
    unnamed x3 -> x1, local copies, waits for them, and re-layouts: 5.25 us -> 1.97 us
    reshape x1 -> x0, local copies, waits for them, and re-layouts: 1.29 us -> none  [local_step(): norm_gain.reshape(1, H)]
where the time goes in v2:
time: 95 us; the launch traced here: 94.8 us
  Pallas kernels  92.8 us (98%)
  local copies, waits for them, and re-layouts  1.97 us (2%)
    pallas_call x1, Pallas kernels, local_step(): pl.pallas_call(functools.partial(moe_kernel, cfg), out_shape=jax.ShapeDty...  92.8 us
    unnamed x1, local copies, waits for them, and re-layouts  1.97 us

profile of v2, /device:TPU:0, one launch (start us, length us, event | category | flops | bytes accessed | tf_op | source)
XLA Modules:
  0.0 94.8 jit_solution(7083762989432464308)
XLA Ops:
  0.0 92.8 %moe_block.1 = bf16[256,1280]{1,0:T(8,128)(2,1)} custom-call(bf16[256,1280]{1,0:T(8,128)(2,1)} %hid.1, f32[1280]{0:T(1024)} %gain.1, bf16[64,1280]{1,0:T(8,128)(2,1)} %bitcast.4, s32[6,256]{1,0:T(8,128)} %bitcast.5, bf16[8,1280,896]{2,1,0:T(8,128)(2,1)} %wg.1, bf16[8,1280,896]{2,1,0:T(8,128)(2,1)} %wu.1, bf16[8,896,1280]{2,1,0:T(8,128)(2,1)} %wd.1, ...), custom_call_target="tpu_custom_call" | custom-call | tf_op jit(solution)/shard_map/moe_block/pallas_call | solution.py:355
  92.8 2.0 %copy.12 = bf16[256,1280]{1,0:T(8,128)(2,1)} copy(bf16[256,1280]{1,0:T(8,128)(2,1)} %moe_block.1) | data formatting | bytes 1310720

commit v3 on v2

--- a/solution.py
+++ b/solution.py
@@ -15,7 +15,7 @@
 OWN, XN, YN, DG = 0, 1, 2, 3
 SR_SLOT = {XN: 0, YN: 1, DG: 2, OWN: 0}
 SS_SLOT = {XN: 0, YN: 1, DG: 0, OWN: 1}
-NAG = 10
+NAG = 13
 PEERS = [(q, r) for q in range(4) for r in range(2) if (q, r) != (0, 0)]
 
 
@@ -24,8 +24,8 @@
 
 
 def moe_kernel(cfg, hid, gain, rwt, topkt, wg, wu, wd, sg, su, sd, out,
-               gu, dn, g, wloc, win, rankm, x, act, o, comb, ash, acc, ss, sr, s, rx, ry, qx, qy,
-               gu_sem, dn_sem, ag_s, ag_r, sib_s, sib_r, ici_s, ici_r):
+               gu, dn, g, wloc, win, rankm, x, act, o, comb, ash, acc, ss, sr, s, rx, ry, qx, qy, fin,
+               gu_sem, dn_sem, out_sem, ag_s, ag_r, sib_s, sib_r, ici_s, ici_r):
     T, H, FF, EL, SLOT, NB, BW, NS = cfg
     HT = T // 2
     me = lax.axis_index("ep")
@@ -39,20 +39,20 @@
                                             device_id={"ep": ep_of(q, r)}, device_id_type=MESH)
 
     lo, hi = pl.ds(0, HT), pl.ds(HT, HT)
-    qa, qb = 1 + core, 2 - core
-    ha = pl.ds(pl.multiple_of(core * HT, HT), HT)
-    hb = pl.ds(pl.multiple_of((1 - core) * HT, HT), HT)
     ag = {
         0: (g.at[OWN, 0], g.at[OWN, 1], OWN, 1),
-        1: (g.at[OWN, 0, lo], g.at[qa, 0, lo], qa, 0),
-        2: (g.at[OWN, 0, hi], g.at[qa, 0, hi], qa, 0),
-        3: (g.at[OWN, 0], g.at[qb, 0], qb, 0),
-        4: (g.at[qa, 0, ha], g.at[DG, 0, ha], qb, 0),
-        5: (g.at[qb, 0, hb], g.at[DG, 0, hb], qa, 0),
-        6: (g.at[qa, 0], g.at[qa, 1], OWN, 1),
-        7: (g.at[qb, 0], g.at[qb, 1], OWN, 1),
-        8: (g.at[DG, 0, ha], g.at[DG, 1, ha], OWN, 1),
-        9: (g.at[DG, 0, hb], g.at[DG, 1, hb], OWN, 1),
+        1: (g.at[OWN, 0, lo], g.at[XN, 0, lo], XN, 0),
+        2: (g.at[OWN, 0, hi], g.at[YN, 0, hi], YN, 0),
+        3: (g.at[OWN, 0, hi], g.at[XN, 0, hi], XN, 0),
+        4: (g.at[OWN, 0, lo], g.at[YN, 0, lo], YN, 0),
+        5: (g.at[XN, 0, lo], g.at[DG, 0, lo], YN, 0),
+        6: (g.at[YN, 0, hi], g.at[DG, 0, hi], XN, 0),
+        7: (g.at[XN, 0, lo], g.at[XN, 1, lo], OWN, 1),
+        8: (g.at[YN, 0, hi], g.at[YN, 1, hi], OWN, 1),
+        9: (g.at[XN, 0, hi], g.at[XN, 1, hi], OWN, 1),
+        10: (g.at[YN, 0, lo], g.at[YN, 1, lo], OWN, 1),
+        11: (g.at[DG, 0, lo], g.at[DG, 1, lo], OWN, 1),
+        12: (g.at[DG, 0, hi], g.at[DG, 1, hi], OWN, 1),
     }
     for j, (q, r) in enumerate(PEERS):
         ag[NAG + j] = (wloc.at[ep_of(q, r)], win.at[q, r], q, r)
@@ -86,15 +86,16 @@
         return pltpu.make_async_copy(sd.at[:, :, pl.ds(pl.multiple_of(n * BW, BW), BW)], dn.at[slot, pl.ds(0, 2)],
                                      dn_sem.at[slot])
 
+    def out_copy(n):
+        cols = pl.ds(n * BW, BW)
+        return pltpu.make_async_copy(fin.at[:, cols], out.at[:, cols], out_sem.at[n])
+
     sg_load = pltpu.make_async_copy(sg, gu.at[NS - 2], gu_sem.at[NS - 2, 0])
     su_load = pltpu.make_async_copy(su, gu.at[NS - 1], gu_sem.at[NS - 1, 0])
     sg_load.start()
     su_load.start()
     sd_load(0, 0).start()
     sd_load(1, 1).start()
-    for e in range(NS - 2):
-        for c in gu_loads(e, e):
-            c.start()
 
     barrier = pltpu.get_barrier_semaphore()
     for q, r in PEERS:
@@ -103,9 +104,6 @@
     h = hid[...].astype(F32)
     inv = lax.rsqrt(jnp.mean(h * h, axis=-1, keepdims=True) + NORM_EPS)
     g[OWN, 0] = (h * inv * gain[...][None, :]).astype(BF16)
-    pl.semaphore_wait(barrier, len(PEERS))
-    agc(1).start()
-    agc(0).start()
 
     logits = lax.dot_general(rwt[...], g[OWN, 0], (((1,), (1,)), ((), ())), preferred_element_type=F32)
     ex = jnp.exp(logits - jnp.max(logits, axis=0, keepdims=True))
@@ -115,13 +113,20 @@
     for j in range(1, topkt.shape[0]):
         chosen = jnp.logical_or(chosen, topkt[j:j + 1, :] == expert)
     wloc[...] = jnp.where(chosen, p, -1.0).reshape(8, EL, T)
+    pl.semaphore_wait(barrier, len(PEERS))
+    agc(1).start()
+    agc(2).start()
     for j in range(len(PEERS)):
         agc(NAG + j).start()
-    agc(2).start()
+    for k in (0, 3, 4):
+        agc(k).start()
     win[OWN, 0] = wloc[me]
 
     sg_load.wait()
     su_load.wait()
+    for e in range(NS - 2):
+        for c in gu_loads(e, e):
+            c.start()
 
     @pl.loop(0, ash.shape[1] // BW)
     def _(n):
@@ -148,14 +153,6 @@
         @pl.when(n + 2 >= NB)
         def _():
             dn_load(n + 2 - NB, slot).start()
-
-    agc(1).wait_send()
-    agc(2).wait_send()
-    agc(3).start()
-    agc(1).wait_recv()
-    agc(2).wait_recv()
-    agc(6).start()
-    agc(4).start()
 
     for j in range(len(PEERS)):
         agc(NAG + j).wait_recv()
@@ -171,17 +168,14 @@
 
     def dispatch(q, r, i):
         pick = jnp.where(hits(q, r), 1.0, 0.0).reshape(EL * SLOT, T).astype(BF16)
-        x[:, i] = dot(pick, g[q, r]).astype(BF16).reshape(EL, SLOT, H)
+        x[:, pl.ds(pl.multiple_of(i * SLOT, SLOT), SLOT)] = dot(pick, g[q, r]).reshape(EL, SLOT, H)
 
     def build_comb(q, r, i):
         w = jnp.broadcast_to(win[q, r][:, None, :], (EL, SLOT, T))
-        cw = jnp.where(hits(q, r), w, 0.0).reshape(EL * SLOT, T).T
-        c1 = cw.astype(BF16)
-        rest = cw - c1.astype(F32)
-        c2 = rest.astype(BF16)
-        comb[i, 0] = c1
-        comb[i, 1] = c2
-        comb[i, 2] = (rest - c2.astype(F32)).astype(BF16)
+        cw = jnp.where(hits(q, r), w, 0.0).reshape(EL * SLOT, T)
+        c1 = cw.astype(BF16).astype(F32)
+        c2 = (cw - c1).astype(BF16).astype(F32)
+        comb[i] = jnp.concatenate([c1, c2, cw - c1 - c2], axis=0).T.astype(BF16)
 
     def finish(q, n):
         sibc(q, n).wait_recv()
@@ -205,8 +199,10 @@
         s[XN - 1, n, hi] = s[XN - 1, n, hi] + qy[n]
         icic(5, n).start()
 
-    def gate_up(p, a0, a1, step):
-        @pl.loop(0, EL)
+    def gate_up(p, chips, step):
+        rows = 2 * len(chips) * SLOT
+
+        @pl.loop(0, EL, unroll=2)
         def _(i):
             e = EL - 1 - i if p % 2 else i
             slot = e % NS
@@ -216,10 +212,8 @@
                 for c in gu_loads(e, slot):
                     c.wait()
 
-            gua = dot(x[e].reshape(2 * SLOT, H), gu[slot])
-            res = (jax.nn.silu(gua[:, 0:FF]) * gua[:, FF:2 * FF]).astype(BF16)
-            act[e, a0] = res[0:SLOT]
-            act[e, a1] = res[SLOT:2 * SLOT]
+            gua = dot(x[e, 0:rows].astype(BF16), gu[slot])
+            act[e, 0:rows] = (jax.nn.silu(gua[:, 0:FF]) * gua[:, FF:2 * FF]).astype(BF16)
 
             @pl.when(i < EL - NS)
             def _():
@@ -236,8 +230,9 @@
             slot = (n + NB * (p + 1)) % 2
             dn_load(n, slot).wait()
             for e in range(EL):
-                res = dot(act[e, 0:owners].reshape(owners * SLOT, FF), dn[slot, e]).astype(BF16)
-                o[0:owners, e] = res.reshape(owners, SLOT, BW)
+                res = dot(act[e, 0:owners * SLOT], dn[slot, e])
+                for i in range(owners):
+                    o[i, e * SLOT:(e + 1) * SLOT] = res[i * SLOT:(i + 1) * SLOT]
 
             @pl.when(jnp.logical_or(n + 2 < NB, p < 2))
             def _():
@@ -245,8 +240,8 @@
 
             for i in sorted(range(owners), key=lambda i: -(i % 2)):
                 q = chips[i // 2]
-                oo = o[i].reshape(EL * SLOT, BW)
-                part = dot(comb[i, 0], oo) + dot(comb[i, 1], oo) + dot(comb[i, 2], oo)
+                oo = o[i].astype(BF16)
+                part = dot(comb[4 + i if q == DG else i], jnp.concatenate([oo, oo, oo], axis=0))
                 if i % 2:
                     if p:
                         sibc(XN if p == 1 else YN, n).wait_send()
@@ -269,38 +264,32 @@
 
     nothing = lambda i: None
 
+    @pl.loop(0, 6)
+    def _(i):
+        build_comb(1 + i // 2, i % 2, i)
+
+    for k, then in ((1, (7, 5)), (2, (8, 6)), (3, (9,)), (4, (10,))):
+        agc(k).wait_recv()
+        for c in then:
+            agc(c).start()
+    for k in (7, 8, 9, 10):
+        agc(k).wait_recv()
+
     @pl.loop(0, 4)
     def _(i):
-        build_comb(1 + i // 2, i % 2, i)
-
-    def second_arrival(i):
-        @pl.when(i == 6)
-        def _():
-            agc(3).wait_recv()
-            agc(7).start()
-            agc(5).start()
-
-    agc(6).wait_recv()
-    dispatch(qa, 0, 0)
-    dispatch(qb, 1, 1)
-    gate_up(0, 2 * (qa - 1), 2 * (qb - 1) + 1, second_arrival)
-    agc(7).wait_recv()
-    dispatch(qb, 0, 0)
-    dispatch(qa, 1, 1)
-    gate_up(1, 2 * (qb - 1), 2 * (qa - 1) + 1, nothing)
-    agc(4).wait_recv()
-    agc(8).start()
-    agc(5).wait_recv()
-    agc(9).start()
+        dispatch(1 + i // 2, i % 2, i)
+
+    gate_up(0, [XN, YN], nothing)
+    for k, then in ((5, 11), (6, 12)):
+        agc(k).wait_recv()
+        agc(then).start()
     down(0, [XN, YN], nothing)
 
-    for r in range(2):
-        build_comb(DG, r, r)
-    agc(8).wait_recv()
-    agc(9).wait_recv()
+    agc(11).wait_recv()
+    agc(12).wait_recv()
     for r in range(2):
         dispatch(DG, r, r)
-    gate_up(2, 0, 1, nothing)
+    gate_up(1, [DG], nothing)
     down(1, [DG], nothing)
 
     def relay_gu(i):
@@ -321,17 +310,19 @@
     for r in range(2):
         build_comb(OWN, r, r)
         dispatch(OWN, r, r)
-    gate_up(3, 0, 1, relay_gu)
+    gate_up(2, [OWN], relay_gu)
     down(2, [OWN], relay_dn)
 
     for n in range(NB):
         for k in (0, 5, 1, 4):
             icic(k, n).wait_recv()
-        out[:, n * BW:(n + 1) * BW] = (acc[n] + rx[n] + ry[n]).astype(BF16)
+        fin[:, n * BW:(n + 1) * BW] = (acc[n] + rx[n] + ry[n]).astype(BF16)
+        out_copy(n).start()
+    for n in range(NB):
+        out_copy(n).wait()
 
     for k in range(NAG + len(PEERS)):
-        if k not in (1, 2):
-            agc(k).wait_send()
+        agc(k).wait_send()
     for n in range(NB):
         for q in (DG, OWN):
             sibc(q, n).wait_send()
@@ -345,8 +336,8 @@
         EL, _, FF = w_gate.shape
         BW = 256
         NB = H // BW
-        SLOT = 48
-        NS = 5
+        SLOT = 40
+        NS = 4
         cfg = (T, H, FF, EL, SLOT, NB, BW, NS)
         vm = pl.BlockSpec(memory_space=pltpu.VMEM)
         anym = pl.BlockSpec(memory_space=pl.ANY)
@@ -356,7 +347,7 @@
             functools.partial(moe_kernel, cfg),
             out_shape=jax.ShapeDtypeStruct((T, H), BF16),
             in_specs=[vm, vm, vm, vm] + [anym] * 6,
-            out_specs=vm,
+            out_specs=anym,
             scratch_shapes=[
                 pltpu.VMEM((NS, H, 2 * FF), BF16),
                 pltpu.VMEM((2, EL, FF, BW), BF16),
@@ -364,10 +355,10 @@
                 pltpu.VMEM((8, EL, T), F32),
                 pltpu.VMEM((4, 2, EL, T), F32),
                 pltpu.VMEM((4, 2, EL, T), F32),
-                pltpu.VMEM((EL, 2, SLOT, H), BF16),
-                pltpu.VMEM((EL, 4, SLOT, FF), BF16),
-                pltpu.VMEM((4, EL, SLOT, BW), BF16),
-                pltpu.VMEM((4, 3, T, EL * SLOT), BF16),
+                pltpu.VMEM((EL, 4 * SLOT, H), F32),
+                pltpu.VMEM((EL, 4 * SLOT, FF), BF16),
+                pltpu.VMEM((4, EL * SLOT, BW), F32),
+                pltpu.VMEM((6, T, 3 * EL * SLOT), BF16),
                 pltpu.VMEM((T, 2 * FF), BF16),
                 pltpu.VMEM((NB, T, BW), F32),
                 pltpu.VMEM((2, NB, T, BW), F32),
@@ -377,7 +368,8 @@
                 pltpu.VMEM((NB, T, BW), F32),
                 pltpu.VMEM((NB, T // 2, BW), F32),
                 pltpu.VMEM((NB, T // 2, BW), F32),
-                dma((NS, 2)), dma((2,)),
+                pltpu.VMEM((T, H), BF16),
+                dma((NS, 2)), dma((2,)), dma((NB,)),
                 dma((n_ag,)), dma((n_ag,)), dma((4, NB)), dma((4, NB)), dma((6, NB)), dma((6, NB)),
             ],
             compiler_params=pltpu.CompilerParams(collective_id=0, has_side_effects=True, vmem_limit_bytes=67043328),

time: 95 us -> 91.6 us (0.964)
  Pallas kernels: 92.8 us -> 89.5 us
    pallas_call x1, Pallas kernels: 92.8 us -> 89.5 us  [local_step(): pl.pallas_call(functools.partial(moe_kernel, cfg), out_shape=jax.ShapeDty...]
where the time goes in v3:
time: 91.6 us; the launch traced here: 91.4 us
  Pallas kernels  89.5 us (98%)
  local copies, waits for them, and re-layouts  1.97 us (2%)
    pallas_call x1, Pallas kernels, local_step(): pl.pallas_call(functools.partial(moe_kernel, cfg), out_shape=jax.ShapeDty...  89.5 us
    unnamed x1, local copies, waits for them, and re-layouts  1.97 us

profile of v3, /device:TPU:0, one launch (start us, length us, event | category | flops | bytes accessed | tf_op | source)
XLA Modules:
  0.0 91.4 jit_solution(14434089372152184463)
XLA Ops:
  0.0 89.5 %moe_block.1 = bf16[256,1280]{1,0:T(8,128)(2,1)} custom-call(bf16[256,1280]{1,0:T(8,128)(2,1)} %hid.1, f32[1280]{0:T(1024)} %gain.1, bf16[64,1280]{1,0:T(8,128)(2,1)} %bitcast.4, s32[6,256]{1,0:T(8,128)} %bitcast.5, bf16[8,1280,896]{2,1,0:T(8,128)(2,1)} %wg.1, bf16[8,1280,896]{2,1,0:T(8,128)(2,1)} %wu.1, bf16[8,896,1280]{2,1,0:T(8,128)(2,1)} %wd.1, ...), custom_call_target="tpu_custom_call" | custom-call | tf_op jit(solution)/shard_map/moe_block/pallas_call | solution.py:346
  89.5 2.0 %copy.12 = bf16[256,1280]{1,0:T(8,128)(2,1)} copy(bf16[256,1280]{1,0:T(8,128)(2,1)} %moe_block.1) | data formatting | bytes 1310720

commit v4 on v3

--- a/solution.py
+++ b/solution.py
@@ -13,7 +13,7 @@
 BF16 = jnp.bfloat16
 
 OWN, XN, YN, DG = 0, 1, 2, 3
-SR_SLOT = {XN: 0, YN: 1, DG: 2, OWN: 0}
+SR_SLOT = {XN: 0, YN: 1, DG: 2, OWN: 2}
 SS_SLOT = {XN: 0, YN: 1, DG: 0, OWN: 1}
 NAG = 13
 PEERS = [(q, r) for q in range(4) for r in range(2) if (q, r) != (0, 0)]
@@ -24,8 +24,8 @@
 
 
 def moe_kernel(cfg, hid, gain, rwt, topkt, wg, wu, wd, sg, su, sd, out,
-               gu, dn, g, wloc, win, rankm, x, act, o, comb, ash, acc, ss, sr, s, rx, ry, qx, qy, fin,
-               gu_sem, dn_sem, out_sem, ag_s, ag_r, sib_s, sib_r, ici_s, ici_r):
+               gu, dn, g, wloc, win, rankm, x, act, comb, ash, acc, ss, sr, s, rx, ry, qx, qy, fin, oall,
+               gu_sem, dn_sem, out_sem, ag_s, ag_r, sib_s, sib_r, sbh_s, sbh_r, ici_s, ici_r):
     T, H, FF, EL, SLOT, NB, BW, NS = cfg
     HT = T // 2
     me = lax.axis_index("ep")
@@ -64,6 +64,12 @@
     def sibc(q, n):
         return rcopy(ss.at[SS_SLOT[q], n], sr.at[SR_SLOT[q], n], sib_s.at[q, n], sib_r.at[q, n], OWN, 1)
 
+    direct = {XN: lo, YN: hi}
+    later = {XN: hi, YN: lo}
+
+    def sibh(q, n, half, b):
+        return rcopy(ss.at[q - 1, n, half], sr.at[q - 1, n, half], sbh_s.at[b, q - 1, n], sbh_r.at[b, q - 1, n], OWN, 1)
+
     def icic(k, n):
         src, dst, q = [
             (s.at[XN - 1, n, lo], rx.at[n, lo], XN),
@@ -178,31 +184,43 @@
         comb[i] = jnp.concatenate([c1, c2, cw - c1 - c2], axis=0).T.astype(BF16)
 
     def finish(q, n):
+        if q in direct:
+            half = direct[q]
+            sibh(q, n, half, 0).wait_recv()
+            s[q - 1, n, half] = s[q - 1, n, half] + sr[q - 1, n, half]
+            icic(q - 1, n).start()
+            return
         sibc(q, n).wait_recv()
         if q == OWN:
             acc[n] = acc[n] + sr[SR_SLOT[q], n]
             return
         s[q - 1, n] = s[q - 1, n] + sr[SR_SLOT[q], n]
-        if q == XN:
-            icic(0, n).start()
-        elif q == YN:
-            icic(1, n).start()
-        else:
-            icic(2, n).start()
-            icic(3, n).start()
+        icic(2, n).start()
+        icic(3, n).start()
+
+    def deferred(n):
+        sibc(DG, n).wait_send()
+        for q in (XN, YN):
+            i = 2 * (q - 1) + 1
+            oo = oall[n, i]
+            ss[q - 1, n, later[q]] = dot(comb[i, later[q]], jnp.concatenate([oo, oo, oo], axis=0))
+            sibh(q, n, later[q], 1).start()
+        for q in (XN, YN):
+            i = 2 * (q - 1)
+            oo = oall[n, i]
+            s[q - 1, n, later[q]] = dot(comb[i, later[q]], jnp.concatenate([oo, oo, oo], axis=0))
 
     def relay(n):
-        icic(2, n).wait_recv()
-        s[YN - 1, n, lo] = s[YN - 1, n, lo] + qx[n]
-        icic(4, n).start()
-        icic(3, n).wait_recv()
-        s[XN - 1, n, hi] = s[XN - 1, n, hi] + qy[n]
-        icic(5, n).start()
+        for q, k, buf in ((YN, 2, qx), (XN, 3, qy)):
+            sibh(q, n, later[q], 1).wait_recv()
+            icic(k, n).wait_recv()
+            s[q - 1, n, later[q]] = s[q - 1, n, later[q]] + sr[q - 1, n, later[q]] + buf[n]
+            icic(k + 2, n).start()
 
     def gate_up(p, chips, step):
         rows = 2 * len(chips) * SLOT
 
-        @pl.loop(0, EL, unroll=2)
+        @pl.loop(0, EL)
         def _(i):
             e = EL - 1 - i if p % 2 else i
             slot = e % NS
@@ -232,7 +250,7 @@
             for e in range(EL):
                 res = dot(act[e, 0:owners * SLOT], dn[slot, e])
                 for i in range(owners):
-                    o[i, e * SLOT:(e + 1) * SLOT] = res[i * SLOT:(i + 1) * SLOT]
+                    x[i, e % 4 * SLOT:(e % 4 + 1) * SLOT, e // 4 * BW:(e // 4 + 1) * BW] = res[i * SLOT:(i + 1) * SLOT]
 
             @pl.when(jnp.logical_or(n + 2 < NB, p < 2))
             def _():
@@ -240,11 +258,31 @@
 
             for i in sorted(range(owners), key=lambda i: -(i % 2)):
                 q = chips[i // 2]
-                oo = o[i].astype(BF16)
-                part = dot(comb[4 + i if q == DG else i], jnp.concatenate([oo, oo, oo], axis=0))
+                if i == owners - 2 - 2 * (owners == 4):
+                    @pl.when(n == 1)
+                    def _():
+                        for c in chips:
+                            finish(c, 0)
+
+                oo = jnp.concatenate([x[i, :, 0:BW], x[i, :, BW:2 * BW]], axis=0).astype(BF16)
+                stack = jnp.concatenate([oo, oo, oo], axis=0)
+                if q in direct:
+                    half = direct[q]
+                    oall[n, i] = oo
+                    part = dot(comb[i, half], stack)
+                    if i % 2:
+                        ss[q - 1, n, half] = part
+                        sibh(q, n, half, 0).start()
+                    else:
+                        s[q - 1, n, half] = part
+                    continue
+                part = dot(comb[4 + i], stack)
                 if i % 2:
-                    if p:
-                        sibc(XN if p == 1 else YN, n).wait_send()
+                    if q == DG:
+                        sibh(XN, n, direct[XN], 0).wait_send()
+                    else:
+                        sibh(YN, n, direct[YN], 0).wait_send()
+                        sibh(YN, n, later[YN], 1).wait_send()
                     ss[SS_SLOT[q], n] = part
                     sibc(q, n).start()
                 elif q == OWN:
@@ -252,7 +290,7 @@
                 else:
                     s[q - 1, n] = part
 
-            @pl.when(n > 0)
+            @pl.when(n > 1)
             def _():
                 for q in chips:
                     finish(q, n - 1)
@@ -272,12 +310,12 @@
         agc(k).wait_recv()
         for c in then:
             agc(c).start()
+    dispatch(XN, 0, 0)
+    dispatch(YN, 0, 2)
     for k in (7, 8, 9, 10):
         agc(k).wait_recv()
-
-    @pl.loop(0, 4)
-    def _(i):
-        dispatch(1 + i // 2, i % 2, i)
+    dispatch(XN, 1, 1)
+    dispatch(YN, 1, 3)
 
     gate_up(0, [XN, YN], nothing)
     for k, then in ((5, 11), (6, 12)):
@@ -293,22 +331,22 @@
     down(1, [DG], nothing)
 
     def relay_gu(i):
-        @pl.when(i % 3 == 1)
+        @pl.when(i % 2 == 1)
         def _():
-            relay(i // 3)
+            relay(i // 2)
 
     def relay_dn(n):
         @pl.when(n == 1)
         def _():
-            relay(3)
-
-        @pl.when(n == 4)
-        def _():
             relay(4)
+
+    @pl.loop(0, NB)
+    def _(n):
+        deferred(n)
 
     agc(0).wait_recv()
     for r in range(2):
-        build_comb(OWN, r, r)
+        build_comb(OWN, r, 4 + r)
         dispatch(OWN, r, r)
     gate_up(2, [OWN], relay_gu)
     down(2, [OWN], relay_dn)
@@ -324,8 +362,8 @@
     for k in range(NAG + len(PEERS)):
         agc(k).wait_send()
     for n in range(NB):
-        for q in (DG, OWN):
-            sibc(q, n).wait_send()
+        sibc(OWN, n).wait_send()
+        sibh(XN, n, later[XN], 1).wait_send()
         for k in range(6):
             icic(k, n).wait_send()
 
@@ -357,7 +395,6 @@
                 pltpu.VMEM((4, 2, EL, T), F32),
                 pltpu.VMEM((EL, 4 * SLOT, H), F32),
                 pltpu.VMEM((EL, 4 * SLOT, FF), BF16),
-                pltpu.VMEM((4, EL * SLOT, BW), F32),
                 pltpu.VMEM((6, T, 3 * EL * SLOT), BF16),
                 pltpu.VMEM((T, 2 * FF), BF16),
                 pltpu.VMEM((NB, T, BW), F32),
@@ -369,8 +406,9 @@
                 pltpu.VMEM((NB, T // 2, BW), F32),
                 pltpu.VMEM((NB, T // 2, BW), F32),
                 pltpu.VMEM((T, H), BF16),
+                pltpu.VMEM((NB, 4, EL * SLOT, BW), BF16),
                 dma((NS, 2)), dma((2,)), dma((NB,)),
-                dma((n_ag,)), dma((n_ag,)), dma((4, NB)), dma((4, NB)), dma((6, NB)), dma((6, NB)),
+                dma((n_ag,)), dma((n_ag,)), dma((4, NB)), dma((4, NB)), dma((2, 2, NB)), dma((2, 2, NB)), dma((6, NB)), dma((6, NB)),
             ],
             compiler_params=pltpu.CompilerParams(collective_id=0, has_side_effects=True, vmem_limit_bytes=67043328),
             name="moe_block",

time: 91.6 us -> 88.7 us (0.968)
  Pallas kernels: 89.5 us -> 86.5 us
    pallas_call x1, Pallas kernels: 89.5 us -> 86.5 us  [local_step(): pl.pallas_call(functools.partial(moe_kernel, cfg), out_shape=jax.ShapeDty...]
where the time goes in v4:
time: 88.7 us; the launch traced here: 88.5 us
  Pallas kernels  86.5 us (98%)
  local copies, waits for them, and re-layouts  1.97 us (2%)
    pallas_call x1, Pallas kernels, local_step(): pl.pallas_call(functools.partial(moe_kernel, cfg), out_shape=jax.ShapeDty...  86.5 us
    unnamed x1, local copies, waits for them, and re-layouts  1.97 us

profile of v4, /device:TPU:0, one launch (start us, length us, event | category | flops | bytes accessed | tf_op | source)
XLA Modules:
  0.0 88.5 jit_solution(7887619194383223999)
XLA Ops:
  0.0 86.5 %moe_block.1 = bf16[256,1280]{1,0:T(8,128)(2,1)} custom-call(bf16[256,1280]{1,0:T(8,128)(2,1)} %hid.1, f32[1280]{0:T(1024)} %gain.1, bf16[64,1280]{1,0:T(8,128)(2,1)} %bitcast.4, s32[6,256]{1,0:T(8,128)} %bitcast.5, bf16[8,1280,896]{2,1,0:T(8,128)(2,1)} %wg.1, bf16[8,1280,896]{2,1,0:T(8,128)(2,1)} %wu.1, bf16[8,896,1280]{2,1,0:T(8,128)(2,1)} %wd.1, ...), custom_call_target="tpu_custom_call" | custom-call | tf_op jit(solution)/shard_map/moe_block/pallas_call | solution.py:384
  86.5 2.0 %copy.12 = bf16[256,1280]{1,0:T(8,128)(2,1)} copy(bf16[256,1280]{1,0:T(8,128)(2,1)} %moe_block.1) | data formatting | bytes 1310720

commit v5 on v4

--- a/solution.py
+++ b/solution.py
@@ -306,7 +306,7 @@
     def _(i):
         build_comb(1 + i // 2, i % 2, i)
 
-    for k, then in ((1, (7, 5)), (2, (8, 6)), (3, (9,)), (4, (10,))):
+    for k, then in ((1, (7,)), (2, (8,)), (3, (9,)), (4, (10, 5, 6))):
         agc(k).wait_recv()
         for c in then:
             agc(c).start()

time: 88.7 us -> 88.1 us (level)
  no operation moved by 1% of the time
where the time goes in v5:
time: 88.1 us; the launch traced here: 87.9 us
  Pallas kernels  86 us (98%)
  local copies, waits for them, and re-layouts  1.97 us (2%)
    pallas_call x1, Pallas kernels, local_step(): pl.pallas_call(functools.partial(moe_kernel, cfg), out_shape=jax.ShapeDty...  86 us
    unnamed x1, local copies, waits for them, and re-layouts  1.97 us

profile of v5, /device:TPU:0, one launch (start us, length us, event | category | flops | bytes accessed | tf_op | source)
XLA Modules:
  0.0 87.9 jit_solution(4597539765797313186)
XLA Ops:
  0.0 86.0 %moe_block.1 = bf16[256,1280]{1,0:T(8,128)(2,1)} custom-call(bf16[256,1280]{1,0:T(8,128)(2,1)} %hid.1, f32[1280]{0:T(1024)} %gain.1, bf16[64,1280]{1,0:T(8,128)(2,1)} %bitcast.4, s32[6,256]{1,0:T(8,128)} %bitcast.5, bf16[8,1280,896]{2,1,0:T(8,128)(2,1)} %wg.1, bf16[8,1280,896]{2,1,0:T(8,128)(2,1)} %wu.1, bf16[8,896,1280]{2,1,0:T(8,128)(2,1)} %wd.1, ...), custom_call_target="tpu_custom_call" | custom-call | tf_op jit(solution)/shard_map/moe_block/pallas_call | solution.py:384
  86.0 2.0 %copy.12 = bf16[256,1280]{1,0:T(8,128)(2,1)} copy(bf16[256,1280]{1,0:T(8,128)(2,1)} %moe_block.1) | data formatting | bytes 1310720
